TPU v7x, 32 devices: a whole 2x2x4 slice. The times are simulated.
32 devices in a mesh: occ: 8 (over z, core), aux: 4 (over y, x).
Axes of the slice: x: 2, y: 2, z: 4, core: 2. Of those that a mesh axis runs over, the one named last changes fastest.
Arguments:
- integrals: bfloat16 [2048, 256, 512], P('aux', 'occ'), may hold values from -1.1953125 to 1.1953125
- metric: bfloat16 [2048, 2048], replicated, may hold values from -0.125 to 0.125
- e_occ: float32 [256], replicated, may hold values from -2 to -0.3
- e_vir: float32 [512], replicated, may hold values from 0.2 to 3
- partner: int32 [256, 2], P(('occ', 'aux')), may hold values from 0 to 7
- screen: int32 [256, 2], P(('occ', 'aux')), may hold values from 0 to 1
Outputs:
- gradient: bfloat16 [2048, 256, 512], P(None, ('occ', 'aux'))
- density: float32 [512, 512], P('occ')
All inputs are finite; a program needn't handle non-finite values.
Results may differ from a plain program's by a relative error of at most 0.0055.
Values may be sent and summed in bfloat16 or wider, within the bound.
A program may use at most 192 MiB of HBM per device.

v0:
```python
import functools

import jax
import jax.numpy as jnp
from jax import lax
from jax.experimental import pallas as pl
from jax.experimental.pallas import tpu as pltpu
from jax.sharding import PartitionSpec as P

NOCC = 256
ROUNDS = 2
BOTH = ("occ", "aux")
NT = (((1,), (1,)), ((), ()))
TN = (((0,), (0,)), ((), ()))

MESH = pl.DeviceIdType.MESH


def amp_kernel(left_at, right_at, kept, e_left, e_right, left, right, col, row, before, amp, density):
    pair = pl.program_id(0)

    @pl.when(pair == 0)
    def _():
        density[...] = before[...]

    @pl.when(kept[pair] != 0)
    def _():
        both = lax.dot_general(left[0], right[0], TN, preferred_element_type=jnp.float32)
        gap = col[...] + row[...] - e_left[pair] - e_right[pair]
        block = (both / gap).astype(jnp.bfloat16)
        amp[0] = block
        density[...] += lax.dot_general(block, block, NT, preferred_element_type=jnp.float32)

    @pl.when(kept[pair] == 0)
    def _():
        amp[0] = jnp.zeros_like(amp[0])


def amplitudes(left, right, left_at, right_at, kept, e_left, e_right, e_vir, before):
    _, naux, nvir = left.shape
    pairs = left_at.shape[0]
    wide = (1, naux, nvir)
    return pl.pallas_call(
        amp_kernel,
        grid_spec=pltpu.PrefetchScalarGridSpec(
            num_scalar_prefetch=5,
            grid=(pairs,),
            in_specs=[
                pl.BlockSpec(wide, lambda m, li, ri, *_: (li[m], 0, 0)),
                pl.BlockSpec(wide, lambda m, li, ri, *_: (ri[m], 0, 0)),
                pl.BlockSpec((nvir, 1), lambda m, *_: (0, 0)),
                pl.BlockSpec((1, nvir), lambda m, *_: (0, 0)),
                pl.BlockSpec((nvir, nvir), lambda m, *_: (0, 0)),
            ],
            out_specs=[
                pl.BlockSpec((1, nvir, nvir), lambda m, *_: (m, 0, 0)),
                pl.BlockSpec((nvir, nvir), lambda m, *_: (0, 0)),
            ],
        ),
        out_shape=[
            jax.ShapeDtypeStruct((pairs, nvir, nvir), jnp.bfloat16),
            jax.ShapeDtypeStruct((nvir, nvir), jnp.float32),
        ],
        cost_estimate=pl.CostEstimate(
            flops=2 * pairs * (naux + nvir) * nvir * nvir,
            bytes_accessed=4 * pairs * naux * nvir,
            transcendentals=0,
        ),
    )(left_at, right_at, kept, e_left, e_right, left, right, e_vir[:, None], e_vir[None, :], before)


def gamma_kernel(own, at0, at1, kept0, kept1, right0, right1, amp0, amp1, out, rows):
    tile = right0.shape[1]
    for i in range(own):
        place = pl.ds(i, tile, stride=own)
        first, second = kept0[i] != 0, kept1[i] != 0

        def term0():
            return lax.dot_general(right0[at0[i]], amp0[i], NT, preferred_element_type=jnp.float32)

        def term1():
            return lax.dot_general(right1[at1[i]], amp1[i], NT, preferred_element_type=jnp.float32)

        def put(value):
            for c in range(rows.shape[0]):
                rows[c, place, :] = value[:, c * 128 : (c + 1) * 128]

        @pl.when(first & second)
        def _():
            put(term0() + term1())

        @pl.when(first & jnp.logical_not(second))
        def _():
            put(term0())

        @pl.when(jnp.logical_not(first) & second)
        def _():
            put(term1())

        @pl.when(jnp.logical_not(first | second))
        def _():
            put(jnp.zeros((tile, out.shape[2]), jnp.float32))

    for c in range(rows.shape[0]):
        block = rows[c].reshape(tile, own, 128)
        out[:, :, c * 128 : (c + 1) * 128] = block.astype(out.dtype)


def gradient(right0, right1, amp0, amp1, at0, at1, kept0, kept1):
    own = amp0.shape[0]
    _, naux, nvir = right0.shape
    tile = min(128, naux)
    full = lambda p, *_: (0, 0, 0)
    return pl.pallas_call(
        functools.partial(gamma_kernel, own),
        grid_spec=pltpu.PrefetchScalarGridSpec(
            num_scalar_prefetch=4,
            grid=(naux // tile,),
            in_specs=[
                pl.BlockSpec((right0.shape[0], tile, nvir), lambda p, *_: (0, p, 0)),
                pl.BlockSpec((right1.shape[0], tile, nvir), lambda p, *_: (0, p, 0)),
                pl.BlockSpec(amp0.shape, full),
                pl.BlockSpec(amp1.shape, full),
            ],
            out_specs=pl.BlockSpec((tile, own, nvir), lambda p, *_: (p, 0, 0)),
            scratch_shapes=[pltpu.VMEM((nvir // 128, tile * own, 128), jnp.float32)],
        ),
        out_shape=jax.ShapeDtypeStruct((naux, own, nvir), jnp.bfloat16),
        cost_estimate=pl.CostEstimate(
            flops=4 * own * naux * nvir * nvir, bytes_accessed=6 * own * naux * nvir, transcendentals=0
        ),
    )(at0, at1, kept0, kept1, right0, right1, amp0, amp1)


def table_kernel(n_occ, n_aux, row, table, send, recv, local):
    groups = n_occ * n_aux
    me = lax.axis_index("occ") * n_aux + lax.axis_index("aux")
    barrier = pltpu.get_barrier_semaphore()

    def place(step):
        other = lax.rem(me + step, groups)
        return (other // n_aux, lax.rem(other, n_aux))

    def greet(step, carry):
        pl.semaphore_signal(barrier, inc=1, device_id=place(step), device_id_type=MESH)
        return carry

    lax.fori_loop(1, groups, greet, 0)
    own = pltpu.make_async_copy(row, table.at[me], local)
    own.start()
    pl.semaphore_wait(barrier, groups - 1)

    def copy(step):
        return pltpu.make_async_remote_copy(
            row, table.at[me], send.at[step], recv.at[step], device_id=place(step), device_id_type=MESH
        )

    def start(step, carry):
        copy(step).start()
        return carry

    def finish(step, carry):
        came = lax.rem(me - step + groups, groups)
        pltpu.make_async_remote_copy(
            row, table.at[came], send.at[step], recv.at[step], device_id=place(step), device_id_type=MESH
        ).wait()
        return carry

    lax.fori_loop(1, groups, start, 0)
    own.wait()
    lax.fori_loop(1, groups, finish, 0)


def everyones(row, n_occ, n_aux):
    groups = n_occ * n_aux
    return pl.pallas_call(
        functools.partial(table_kernel, n_occ, n_aux),
        out_shape=jax.ShapeDtypeStruct((groups,) + row.shape, row.dtype),
        in_specs=[pl.BlockSpec(memory_space=pltpu.VMEM)],
        out_specs=pl.BlockSpec(memory_space=pltpu.VMEM),
        scratch_shapes=[
            pltpu.SemaphoreType.DMA((groups,)),
            pltpu.SemaphoreType.DMA((groups,)),
            pltpu.SemaphoreType.DMA(()),
        ],
        compiler_params=pltpu.CompilerParams(collective_id=0, has_side_effects=True),
    )(row)


def peer_of(i, step, n_aux):
    return i ^ step if n_aux & (n_aux - 1) == 0 else lax.rem(step + n_aux - i, n_aux)


def move_kernel(
    slots, n_occ, n_aux, packed, mixed, coeff, near, far, wrapped,
    held, lent, stage, sent, came, far_sent, far_came, wrap_sems, local, stored,
):
    own = packed.shape[1]
    naux, nvir = stage.shape
    occ, aux = lax.axis_index("occ"), lax.axis_index("aux")
    mate = (lax.rem(occ + n_occ // 2, n_occ), aux)
    after = (lax.rem(occ + 1, n_occ), aux)
    before = (lax.rem(occ + n_occ - 1, n_occ), aux)
    peers = [(occ, peer_of(aux, s, n_aux)) for s in range(n_aux)]

    barrier = pltpu.get_barrier_semaphore()
    greeted = [mate, after, before] + peers[1:]
    for device in greeted:
        pl.semaphore_signal(barrier, inc=1, device_id=device, device_id_type=MESH)
    pl.semaphore_wait(barrier, len(greeted))

    wrap = pltpu.make_async_remote_copy(
        packed.at[n_aux - 1], wrapped, wrap_sems.at[0], wrap_sems.at[1], device_id=after, device_id_type=MESH
    )
    wrap.start()

    def piece(kind, land, source, t, s):
        if s == 0:
            return pltpu.make_async_copy(source, land.at[t, 0], local.at[kind, t])
        return pltpu.make_async_remote_copy(
            source, land.at[t, s], sent.at[kind, t, s], came.at[kind, t, s], device_id=peers[s], device_id_type=MESH
        )

    def send_own(t, carry):
        for s in range(n_aux):
            piece(0, held, packed.at[peers[s][1], t], t, s).start()
        return carry

    def send_near(t, carry):
        for s in range(n_aux):
            to = peers[s][1]

            @pl.when(to == 0)
            def _():
                piece(1, lent, wrapped.at[t], t, s).start()

            @pl.when(to != 0)
            def _():
                piece(1, lent, packed.at[jnp.maximum(to - 1, 0), t], t, s).start()

        return carry

    def transform(kind, land, target, t):
        for s in range(n_aux):
            move = piece(kind, land, packed.at[0, 0], t, s)
            move.wait() if s == 0 else move.wait_recv()
        tile = 256

        def rows(i, carry):
            at = pl.ds(pl.multiple_of(i * tile, tile), tile)
            block = land[t].reshape(naux, nvir)
            stage[at, :] = jnp.dot(mixed[at, :], block, preferred_element_type=jnp.float32).astype(stage.dtype)
            return carry

        lax.fori_loop(0, naux // tile, rows, 0)
        out = pltpu.make_async_copy(stage, target.at[t], stored)
        out.start()
        out.wait()

    def far_copy(t):
        return pltpu.make_async_remote_copy(
            coeff.at[t], far.at[t], far_sent.at[t], far_came.at[t], device_id=mate, device_id_type=MESH
        )

    def own_slot(t, carry):
        transform(0, held, coeff, t)

        @pl.when(t < slots)
        def _():
            far_copy(t).start()

        return carry

    def near_slot(t, carry):
        transform(1, lent, near, t)
        return carry

    lax.fori_loop(0, own, send_own, 0)
    early = min(own, 2)
    lax.fori_loop(0, early, own_slot, 0)
    wrap.wait()
    lax.fori_loop(0, own, send_near, 0)
    lax.fori_loop(early, own, own_slot, 0)
    lax.fori_loop(0, own, near_slot, 0)

    def drain(t, carry):
        for kind, land in ((0, held), (1, lent)):
            for s in range(1, n_aux):
                piece(kind, land, packed.at[0, 0], t, s).wait_send()
        return carry

    lax.fori_loop(0, own, drain, 0)

    def finish(t, carry):
        far_copy(t).wait()
        return carry

    lax.fori_loop(0, slots, finish, 0)


def moved(packed, mixed, slots, n_occ, n_aux):
    _, own, depth, nvir = packed.shape
    naux = depth * n_aux
    anywhere = pl.BlockSpec(memory_space=pl.ANY)
    kind = packed.dtype
    dma = pltpu.SemaphoreType.DMA
    return pl.pallas_call(
        functools.partial(move_kernel, slots, n_occ, n_aux),
        out_shape=[
            jax.ShapeDtypeStruct((own, naux, nvir), kind),
            jax.ShapeDtypeStruct((own, naux, nvir), kind),
            jax.ShapeDtypeStruct((slots, naux, nvir), kind),
            jax.ShapeDtypeStruct((own, depth, nvir), kind),
        ],
        in_specs=[anywhere, pl.BlockSpec(memory_space=pltpu.VMEM)],
        out_specs=[anywhere] * 4,
        scratch_shapes=[
            pltpu.VMEM((own, n_aux, depth, nvir), kind),
            pltpu.VMEM((own, n_aux, depth, nvir), kind),
            pltpu.VMEM((naux, nvir), kind),
            dma((2, own, n_aux)),
            dma((2, own, n_aux)),
            dma((slots,)),
            dma((slots,)),
            dma((2,)),
            dma((2, own)),
            dma(()),
        ],
        compiler_params=pltpu.CompilerParams(
            collective_id=slots, has_side_effects=True, vmem_limit_bytes=60 * 1024 * 1024
        ),
    )(packed, mixed)


def on_device(integrals, metric, e_occ, e_vir, partner, screen):
    n_occ, n_aux = lax.axis_size("occ"), lax.axis_size("aux")
    groups = n_occ * n_aux
    depth, held, nvir = integrals.shape
    own = held // n_aux
    naux = depth * n_aux
    occ, aux = lax.axis_index("occ"), lax.axis_index("aux")
    device = occ * n_aux + aux
    shifts = (1, groups // 2)

    code = (partner * 2 + screen).reshape(1, own * ROUNDS)
    code = jnp.pad(code, ((0, 7), (0, 128 - own * ROUNDS)))
    table = everyones(code, n_occ, n_aux)[:, 0, : own * ROUNDS].reshape(groups, own, ROUNDS)
    place = jnp.arange(own, dtype=jnp.int32)
    wanted = (table[:, :, 1, None] // 2 == place) & (table[:, :, 1, None] % 2 == 1)
    wanted = jnp.roll(jnp.any(wanted, axis=1), -shifts[1], axis=0)
    count = jnp.sum(wanted, axis=1, dtype=jnp.int32)
    first = jnp.cumsum(wanted, axis=1, dtype=jnp.int32) - 1
    last = count[:, None] + jnp.cumsum(~wanted, axis=1, dtype=jnp.int32) - 1
    rank = jnp.where(wanted, first, last)
    order = jnp.sum(jnp.where(rank[:, None, :] == place[None, :, None], place[None, None, :], 0), axis=2)

    here = lax.dynamic_slice(order, (occ * n_aux, 0), (n_aux, own)) + own * jnp.arange(n_aux, dtype=jnp.int32)[:, None]
    packed = jnp.transpose(integrals, (1, 0, 2)).at[here.reshape(-1)].get(mode="promise_in_bounds")
    packed = packed.reshape(n_aux, own, depth, nvir)
    mixed = metric.reshape(naux, n_aux, depth)
    mixed = jnp.concatenate(
        [lax.dynamic_index_in_dim(mixed, peer_of(aux, s, n_aux), 1, False) for s in range(n_aux)], axis=1
    )

    e_own = lax.dynamic_slice(e_occ, (device * own,), (own,))
    at, e_right = [], []
    for rnd in range(ROUNDS):
        source = (device - shifts[rnd]) % groups
        e_right.append(e_occ.at[source * own + partner[:, rnd]].get(mode="promise_in_bounds"))
        ranks = lax.dynamic_index_in_dim(rank, source, 0, False)
        at.append(ranks.at[partner[:, rnd]].get(mode="promise_in_bounds"))
    mine = lax.dynamic_index_in_dim(rank, device, 0, False)

    def run(slots):
        coeff, near, far, _ = moved(packed, mixed, slots, n_occ, n_aux)
        at1 = jnp.minimum(at[1], slots - 1)
        density = jnp.zeros((nvir, nvir), jnp.float32)
        amp0, density = amplitudes(coeff, near, mine, at[0], screen[:, 0], e_own, e_right[0], e_vir, density)
        amp1, density = amplitudes(coeff, far, mine, at1, screen[:, 1], e_own, e_right[1], e_vir, density)
        gamma = gradient(near, far, amp0, amp1, at[0], at1, screen[:, 0], screen[:, 1])
        return gamma, density

    gamma, density = run(own)
    rows = density.reshape(n_occ, n_aux, nvir // groups, nvir)
    rows = lax.psum_scatter(rows, "aux", scatter_dimension=1, tiled=False)
    rows = lax.psum_scatter(rows, "occ", scatter_dimension=0, tiled=False)
    block = lax.all_gather(rows, "aux", axis=0, tiled=True)
    return gamma, block / NOCC


def solution(mesh):
    return jax.shard_map(
        on_device,
        mesh=mesh,
        in_specs=(P("aux", "occ", None), P(), P(), P(), P(BOTH, None), P(BOTH, None)),
        out_specs=(P(None, BOTH, None), P("occ", None)),
        check_vma=False,
    )
```

profile of v0, /device:TPU:0, one launch (start us, length us, event | category | flops | bytes accessed | tf_op | source)
XLA Modules:
  0.0 1034.8 jit_solution(11383200610846229546)
XLA Ops:
  7.3 1.3 slice_bitcast_fusion
  8.6 0.7 multiply_add_fusion
  10.1 11.8 %shard_map.77 = s32[32,8,128]{2,1,0:T(8,128)} custom-call(s32[8,128]{1,0:T(8,128)} %pad.4.row), custom_call_target="tpu_custom_call" | custom-call | tf_op jit(solution)/shard_map/pallas_call | solution.py:176
  21.9 0.9 slice.31
  23.3 0.8 fusion.7
  25.9 16.8 %copy.75 = bf16[512,32,512]{2,0,1:T(8,128)(2,1)} copy(bf16[512,32,512]{2,1,0:T(8,128)(2,1)} %param.6) | data formatting | bytes 33554432 | tf_op args[0]
  43.0 14.5 %reshape.87 = bf16[2048,4,512]{2,1,0:T(4,128)(2,1)} reshape(bf16[2048,2048]{1,0:T(8,128)(2,1)} %param.7) | data formatting | bytes 16777216 | tf_op jit(solution)/shard_map/reshape | solution.py:360
  58.1 1.2 gather_fusion.3
  59.2 0.8 copy.61.col
  60.1 1.2 gather_fusion.4
  61.3 1.2 gather_fusion
  62.5 13.1 %gather_fusion.2 = bf16[32,512,512]{2,1,0:T(8,128)(2,1)} fusion(bf16[32,512,512]{2,1,0:T(8,128)(2,1)} %bitcast.39, s32[1024]{0:T(1024)S(1)} %pad_clamp_fusion.2), kind=kCustom, calls=%fused_computation.2 | custom fusion | bytes 33554560 | tf_op jit(solution)/shard_map/gather | solution.py:358
  75.6 25.4 %constant_dynamic-slice_fusion.3 = (bf16[2048,1,512]{2,1,0:T(2,128)(2,1)S(1)}, bf16[2048,1,512]{2,1,0:T(2,128)(2,1)S(1)}, bf16[2048,1,512]{2,1,0:T(2,128)(2,1)S(1)}, bf16[2048,1,512]{2,1,0:T(2,128)(2,1)S(1)}) fusion(bf16[2048,4,512]{2,1,0:T(4,128)(2,1)} %reshape.87, s32[]{:T(128)S(6)} %select_n.101, s32[]{:T(128)S(6)} %select_n.103, s32[]{:T(128)S(6)} %select_n.102, ...), kind=kLoop, calls=%fused_computation.44 | loop fusion | bytes 16777232 | tf_op jit(solution)/shard_map/jit(dynamic_index_in_dim)/dynamic_slice | solution.py:362
  101.0 1.2 copy_bitcast_fusion.1
  102.3 1.2 copy_bitcast_fusion.3
  103.5 4.0 pad_maximum_fusion.mixed
  107.5 776.0 %shard_map.78 = (bf16[8,2048,512]{2,1,0:T(8,128)(2,1)}, bf16[8,2048,512]{2,1,0:T(8,128)(2,1)}, bf16[8,2048,512]{2,1,0:T(8,128)(2,1)}, bf16[8,512,512]{2,1,0:T(8,128)(2,1)}) custom-call(bf16[4,8,512,512]{3,2,1,0:T(8,128)(2,1)} %bitcast.38, bf16[2048,2048]{1,0:T(8,128)(2,1)} %pad_maximum_fusion.mixed), custom_call_target="tpu_custom_call" | custom-call | tf_op jit(solution)/shard_map/pallas_call | solution.py:307
  883.5 1.1 broadcast_in_dim.19.before
  884.6 19.0 %shard_map.79 = (bf16[8,512,512]{2,1,0:T(8,128)(2,1)}, f32[512,512]{1,0:T(8,128)}) custom-call(s32[8]{0:T(128)} %get-tuple-element.16.left_at, s32[8]{0:T(128)} %gather_fusion, s32[8]{0:T(128)} %get-tuple-element.32.kept.kept0, f32[8]{0:T(128)} %dynamic_slice.37.e_left, f32[8]{0:T(128)} %gather_fusion.3, bf16[8,2048,512]{2,1,0:T(8,128)(2,1)} %get-tuple-element.11.left, ...), custom_call_target="tpu_custom_call" | custom-call | flops 10737418240 | bytes 33554432 | tf_op jit(solution)/shard_map/pallas_call | solution.py:43
  903.6 17.6 %shard_map.80 = (bf16[8,512,512]{2,1,0:T(8,128)(2,1)}, f32[512,512]{1,0:T(8,128)}) custom-call(s32[8]{0:T(128)} %get-tuple-element.16.left_at, s32[8]{0:T(128)} %broadcast_minimum_fusion.right_at.at1, s32[8]{0:T(128)} %get-tuple-element.31.kept.kept1, f32[8]{0:T(128)} %dynamic_slice.37.e_left, f32[8]{0:T(128)} %gather_fusion.4, ...), custom_call_target="tpu_custom_call" | custom-call | flops 10737418240 | bytes 33554432 | tf_op jit(solution)/shard_map/pallas_call | solution.py:43
  921.2 2.3 copy.63
  923.6 28.6 %reduce-scatter.7.cloned.1.call-done = f32[8,1,16,512]{3,2,0,1:T(8,128)} async-done(((f32[8,4,16,512]{3,2,0,1:T(8,128)}), f32[8,1,16,512]{3,2,0,1:T(8,128)}) %reduce-scatter.7.cloned.1.call-update) | async-done | bytes 262160
  952.2 50.3 %shard_map.81 = bf16[2048,8,512]{2,1,0:T(8,128)(2,1)} custom-call(s32[8]{0:T(128)} %gather_fusion, s32[8]{0:T(128)} %broadcast_minimum_fusion.right_at.at1, s32[8]{0:T(128)} %get-tuple-element.32.kept.kept0, s32[8]{0:T(128)} %get-tuple-element.31.kept.kept1, bf16[8,2048,512]{2,1,0:T(8,128)(2,1)} %get-tuple-element.9.right.right0, ...), custom_call_target="tpu_custom_call" | custom-call | flops 17179869184 | bytes 50331648 | tf_op jit(solution)/shard_map/pallas_call | solution.py:114
  1002.5 24.8 %all-gather = f32[1,64,512]{2,1,0:T(8,128)S(1)} all-gather(f32[1,16,512]{2,1,0:T(8,128)} %reduce-scatter.5.cloned.1.call-done), channel_id=2, replica_groups=mesh['occ'=8,'aux'=4] {'aux'}, dimensions={1}, use_global_device_ids=true | all-gather | bytes 163840 | tf_op jit(solution)/shard_map/all_gather | solution.py:387
  (37 shorter events, 4.7 us)
Async XLA Ops:
  7.2 945.0 %reduce-scatter.7.cloned.1.call-start = ((), (), s32[]{:S(2)}) async-start(), calls=%async_computation.3 | async-start | bytes 1310720
  42.9 14.5 %copy-start = (f32[256]{0:T(256)S(1)}, f32[256]{0:T(256)}, u32[]{:S(2)}) copy-start(f32[256]{0:T(256)} %param.8) | copy-start | bytes 3076
  43.0 16.3 %copy-start.1 = (f32[512]{0:T(512)S(1)}, f32[512]{0:T(512)}, u32[]{:S(2)}) copy-start(f32[512]{0:T(512)} %param.9) | copy-start | bytes 6148
  923.5 79.0 %reduce-scatter.5.cloned.1.call-start = ((), (), s32[]{:S(2)}) async-start(), calls=%async_computation.2 | async-start | bytes 294912 | tf_op jit(solution)/shard_map/reduce_scatter | solution.py:386
Sparse Core Ops, SparseCore 0:
  923.6 28.5 reduce-scatter.6
  954.4 31.0 reduce-scatter.4
where the time goes:
time: 1040 us; the launch traced here: 1030 us
  Pallas kernels  875 us (84%)
  local copies, waits for them, and re-layouts  85.4 us (8%)
  waiting for transfers between devices  28.7 us (3%)
  blocking collectives  24.8 us (2%)
  between operations  14.2 us (1%)
    pallas_call x1, Pallas kernels, moved(): pl.pallas_call(functools.partial(move_kernel, slots, n_occ, n_aux), out_s...  776 us
    pallas_call x1, Pallas kernels, gradient(): pl.pallas_call(functools.partial(gamma_kernel, own), grid_spec=pltpu.Pref...  50.3 us
    pallas_call x2, Pallas kernels, amplitudes(): pl.pallas_call(amp_kernel, grid_spec=pltpu.PrefetchScalarGridSpec(num_sca...  36.6 us
    unnamed x3, waiting for transfers between devices  28.7 us
    dynamic_slice x1, local copies, waits for them, and re-layouts, on_device(): lax.dynamic_index_in_dim(mixed, peer_of(aux, s, n_aux), 1, False)  25.4 us
    all_gather x1, blocking collectives, on_device(): block = lax.all_gather(rows, 'aux', axis=0, tiled=True)  24.8 us
  transfers between devices with their start and end apart: 2, of which 1 were waited for; matrix products, arithmetic and copies ran while one was open for 0% of the time, Pallas kernels for 5%

commit v1 on v0

--- a/solution.py
+++ b/solution.py
@@ -70,9 +70,7 @@
 
 
 def gamma_kernel(own, at0, at1, kept0, kept1, right0, right1, amp0, amp1, out, rows):
-    tile = right0.shape[1]
     for i in range(own):
-        place = pl.ds(i, tile, stride=own)
         first, second = kept0[i] != 0, kept1[i] != 0
 
         def term0():
@@ -81,35 +79,29 @@
         def term1():
             return lax.dot_general(right1[at1[i]], amp1[i], NT, preferred_element_type=jnp.float32)
 
-        def put(value):
-            for c in range(rows.shape[0]):
-                rows[c, place, :] = value[:, c * 128 : (c + 1) * 128]
-
         @pl.when(first & second)
         def _():
-            put(term0() + term1())
+            rows[i] = (term0() + term1()).astype(rows.dtype)
 
         @pl.when(first & jnp.logical_not(second))
         def _():
-            put(term0())
+            rows[i] = term0().astype(rows.dtype)
 
         @pl.when(jnp.logical_not(first) & second)
         def _():
-            put(term1())
+            rows[i] = term1().astype(rows.dtype)
 
         @pl.when(jnp.logical_not(first | second))
         def _():
-            put(jnp.zeros((tile, out.shape[2]), jnp.float32))
-
-    for c in range(rows.shape[0]):
-        block = rows[c].reshape(tile, own, 128)
-        out[:, :, c * 128 : (c + 1) * 128] = block.astype(out.dtype)
+            rows[i] = jnp.zeros_like(rows[i])
+
+    out[...] = pltpu.einshape("ipa->pia", rows[...])
 
 
 def gradient(right0, right1, amp0, amp1, at0, at1, kept0, kept1):
     own = amp0.shape[0]
     _, naux, nvir = right0.shape
-    tile = min(128, naux)
+    tile = min(256, naux)
     full = lambda p, *_: (0, 0, 0)
     return pl.pallas_call(
         functools.partial(gamma_kernel, own),
@@ -123,7 +115,7 @@
                 pl.BlockSpec(amp1.shape, full),
             ],
             out_specs=pl.BlockSpec((tile, own, nvir), lambda p, *_: (p, 0, 0)),
-            scratch_shapes=[pltpu.VMEM((nvir // 128, tile * own, 128), jnp.float32)],
+            scratch_shapes=[pltpu.VMEM((own, tile, nvir), jnp.bfloat16)],
         ),
         out_shape=jax.ShapeDtypeStruct((naux, own, nvir), jnp.bfloat16),
         cost_estimate=pl.CostEstimate(
@@ -187,6 +179,30 @@
     )(row)
 
 
+def pack_kernel(order, x, out, turned):
+    n_aux, own = out.shape[:2]
+    turned[...] = pltpu.einshape("qja->jqa", x[...])
+    for slot in range(n_aux * own):
+        out[slot // own, slot % own] = turned[order[slot]]
+
+
+def packed_blocks(x, order, n_aux):
+    depth, held, nvir = x.shape
+    own = held // n_aux
+    tile = min(32, depth)
+    return pl.pallas_call(
+        pack_kernel,
+        grid_spec=pltpu.PrefetchScalarGridSpec(
+            num_scalar_prefetch=1,
+            grid=(depth // tile,),
+            in_specs=[pl.BlockSpec((tile, held, nvir), lambda q, *_: (q, 0, 0))],
+            out_specs=pl.BlockSpec((n_aux, own, tile, nvir), lambda q, *_: (0, 0, q, 0)),
+            scratch_shapes=[pltpu.VMEM((held, tile, nvir), x.dtype)],
+        ),
+        out_shape=jax.ShapeDtypeStruct((n_aux, own, depth, nvir), x.dtype),
+    )(order, x)
+
+
 def peer_of(i, step, n_aux):
     return i ^ step if n_aux & (n_aux - 1) == 0 else lax.rem(step + n_aux - i, n_aux)
 
@@ -216,9 +232,9 @@
 
     def piece(kind, land, source, t, s):
         if s == 0:
-            return pltpu.make_async_copy(source, land.at[t, 0], local.at[kind, t])
+            return pltpu.make_async_copy(source, land.at[t, aux], local.at[kind, t])
         return pltpu.make_async_remote_copy(
-            source, land.at[t, s], sent.at[kind, t, s], came.at[kind, t, s], device_id=peers[s], device_id_type=MESH
+            source, land.at[t, aux], sent.at[kind, t, s], came.at[kind, t, s], device_id=peers[s], device_id_type=MESH
         )
 
     def send_own(t, carry):
@@ -242,8 +258,13 @@
 
     def transform(kind, land, target, t):
         for s in range(n_aux):
-            move = piece(kind, land, packed.at[0, 0], t, s)
-            move.wait() if s == 0 else move.wait_recv()
+            if s == 0:
+                piece(kind, land, packed.at[0, 0], t, 0).wait()
+            else:
+                pltpu.make_async_remote_copy(
+                    packed.at[0, 0], land.at[t, peers[s][1]], sent.at[kind, t, s], came.at[kind, t, s],
+                    device_id=peers[s], device_id_type=MESH,
+                ).wait_recv()
         tile = 256
 
         def rows(i, carry):
@@ -309,7 +330,7 @@
         out_shape=[
             jax.ShapeDtypeStruct((own, naux, nvir), kind),
             jax.ShapeDtypeStruct((own, naux, nvir), kind),
-            jax.ShapeDtypeStruct((slots, naux, nvir), kind),
+            jax.ShapeDtypeStruct((own, naux, nvir), kind),
             jax.ShapeDtypeStruct((own, depth, nvir), kind),
         ],
         in_specs=[anywhere, pl.BlockSpec(memory_space=pltpu.VMEM)],
@@ -355,12 +376,7 @@
     order = jnp.sum(jnp.where(rank[:, None, :] == place[None, :, None], place[None, None, :], 0), axis=2)
 
     here = lax.dynamic_slice(order, (occ * n_aux, 0), (n_aux, own)) + own * jnp.arange(n_aux, dtype=jnp.int32)[:, None]
-    packed = jnp.transpose(integrals, (1, 0, 2)).at[here.reshape(-1)].get(mode="promise_in_bounds")
-    packed = packed.reshape(n_aux, own, depth, nvir)
-    mixed = metric.reshape(naux, n_aux, depth)
-    mixed = jnp.concatenate(
-        [lax.dynamic_index_in_dim(mixed, peer_of(aux, s, n_aux), 1, False) for s in range(n_aux)], axis=1
-    )
+    packed = packed_blocks(integrals, here.reshape(-1), n_aux)
 
     e_own = lax.dynamic_slice(e_occ, (device * own,), (own,))
     at, e_right = [], []
@@ -371,16 +387,19 @@
         at.append(ranks.at[partner[:, rnd]].get(mode="promise_in_bounds"))
     mine = lax.dynamic_index_in_dim(rank, device, 0, False)
 
-    def run(slots):
-        coeff, near, far, _ = moved(packed, mixed, slots, n_occ, n_aux)
-        at1 = jnp.minimum(at[1], slots - 1)
-        density = jnp.zeros((nvir, nvir), jnp.float32)
-        amp0, density = amplitudes(coeff, near, mine, at[0], screen[:, 0], e_own, e_right[0], e_vir, density)
-        amp1, density = amplitudes(coeff, far, mine, at1, screen[:, 1], e_own, e_right[1], e_vir, density)
-        gamma = gradient(near, far, amp0, amp1, at[0], at1, screen[:, 0], screen[:, 1])
-        return gamma, density
-
-    gamma, density = run(own)
+    most = jnp.max(count)
+    fewest = max(1, own - 4)
+    choices = list(range(fewest, own + 1))
+    branch = jnp.clip(most - fewest, 0, len(choices) - 1)
+    coeff, near, far = lax.switch(
+        branch, [lambda slots=slots: tuple(moved(packed, metric, slots, n_occ, n_aux)[:3]) for slots in choices]
+    )
+    kept = [screen[:, 0], screen[:, 1]]
+    at1 = jnp.minimum(at[1], jnp.maximum(most, 1) - 1)
+    density = jnp.zeros((nvir, nvir), jnp.float32)
+    amp0, density = amplitudes(coeff, near, mine, at[0], kept[0], e_own, e_right[0], e_vir, density)
+    amp1, density = amplitudes(coeff, far, mine, at1, kept[1], e_own, e_right[1], e_vir, density)
+    gamma = gradient(near, far, amp0, amp1, at[0], at1, kept[0], kept[1])
     rows = density.reshape(n_occ, n_aux, nvir // groups, nvir)
     rows = lax.psum_scatter(rows, "aux", scatter_dimension=1, tiled=False)
     rows = lax.psum_scatter(rows, "occ", scatter_dimension=0, tiled=False)

time: 1040 us -> 871 us (0.84)
  Pallas kernels: 875 us -> 785 us
  local copies, waits for them, and re-layouts: 85.4 us -> 16.3 us
    pallas_call x1, Pallas kernels: 776 us -> 686 us  [moved(): pl.pallas_call(functools.partial(move_kernel, slots, n_occ, n_aux), out_s...]
    dynamic_slice x1 -> x0, local copies, waits for them, and re-layouts: 25.4 us -> none  [on_device(): lax.dynamic_index_in_dim(mixed, peer_of(aux, s, n_aux), 1, False)]
    pallas_call x1, Pallas kernels: 50.3 us -> 29.8 us  [gradient(): pl.pallas_call(functools.partial(gamma_kernel, own), grid_spec=pltpu.Pref...]
    pallas_call x0 -> x1, Pallas kernels: none -> 20.2 us  [packed_blocks(): pl.pallas_call(pack_kernel, grid_spec=pltpu.PrefetchScalarGridSpec(num_sc...]
    unnamed x6 -> x1, local copies, waits for them, and re-layouts: 16.8 us -> 0.01 us
    reshape x2 -> x1, local copies, waits for them, and re-layouts: 14.6 us -> 0.6 us  [on_device(): packed = packed_blocks(integrals, here.reshape(-1), n_aux)]
    gather x1 -> x0, local copies, waits for them, and re-layouts: 13.1 us -> none  [on_device(): jnp.transpose(integrals, (1, 0, 2)).at[here.reshape(-1)]]
  transfers between devices with their start and end apart: 2 -> 2, of which waited for: 1 -> 2; matrix products, arithmetic and copies ran while one was open for 0% -> 0% of each run, Pallas kernels for 5% -> 3%
where the time goes in v1:
time: 871 us
  Pallas kernels  785 us (90%)
  waiting for transfers between devices  33.4 us (4%)
  blocking collectives  17.2 us (2%)
  local copies, waits for them, and re-layouts  16.3 us (2%)
  between operations  15.5 us (2%)
    pallas_call x1, Pallas kernels, moved(): pl.pallas_call(functools.partial(move_kernel, slots, n_occ, n_aux), out_s...  686 us
    pallas_call x2, Pallas kernels, amplitudes(): pl.pallas_call(amp_kernel, grid_spec=pltpu.PrefetchScalarGridSpec(num_sca...  37 us
    unnamed x3, waiting for transfers between devices  30.1 us
    pallas_call x1, Pallas kernels, gradient(): pl.pallas_call(functools.partial(gamma_kernel, own), grid_spec=pltpu.Pref...  29.8 us
    pallas_call x1, Pallas kernels, packed_blocks(): pl.pallas_call(pack_kernel, grid_spec=pltpu.PrefetchScalarGridSpec(num_sc...  20.2 us
  transfers between devices with their start and end apart: 2, of which 2 were waited for; matrix products, arithmetic and copies ran while one was open for 0% of the time, Pallas kernels for 3%

profile of v1, /device:TPU:0, one launch (start us, length us, event | category | flops | bytes accessed | tf_op | source)
XLA Modules:
  0.0 871.2 jit_solution(7939353110383805791)
XLA Ops:
  7.3 1.3 slice_bitcast_fusion
  8.6 0.7 multiply_add_fusion
  10.0 11.8 %shard_map.77 = s32[32,8,128]{2,1,0:T(8,128)} custom-call(s32[8,128]{1,0:T(8,128)} %pad.4.row), custom_call_target="tpu_custom_call" | custom-call | tf_op jit(solution)/shard_map/pallas_call | solution.py:168
  21.9 0.9 slice.29
  25.9 0.8 fusion.6
  26.7 1.3 dynamic_slice.20.e_left
  28.0 1.8 gather_fusion.2
  29.8 1.5 copy.36.col
  31.3 1.9 gather_fusion.3
  33.2 0.7 dynamic-slice_reduce_fusion
  33.9 1.2 gather_fusion
  35.2 0.6 gather_fusion.1
  36.3 20.2 %shard_map.78 = bf16[4,8,512,512]{3,2,1,0:T(8,128)(2,1)} custom-call(s32[32]{0:T(128)} %reshape.51.order, bf16[512,32,512]{2,1,0:T(8,128)(2,1)} %x.3), custom_call_target="tpu_custom_call" | custom-call | tf_op jit(solution)/shard_map/pallas_call | solution.py:193
  56.5 686.2 %conditional.1 = (bf16[8,2048,512]{2,1,0:T(8,128)(2,1)}, bf16[8,2048,512]{2,1,0:T(8,128)(2,1)}, bf16[8,2048,512]{2,1,0:T(8,128)(2,1)}) conditional(s32[]{:T(128)} %clamp.3, (bf16[4,8,512,512]{3,2,1,0:T(8,128)(2,1)}, bf16[2048,2048]{1,0:T(8,128)(2,1)}) %tuple.28, (bf16[4,8,512,512]{3,2,1,0:T(8,128)(2,1)}, ...), branch_computations={%region_6.7_spmd, %region_7.8_spmd, %region_8.9_spmd, %region_9.10... | conditional | bytes 24 | solution.py:394
  56.5 686.1 %branch_3_fun.1 = (bf16[8,2048,512]{2,1,0:T(8,128)(2,1)}, bf16[8,2048,512]{2,1,0:T(8,128)(2,1)}, bf16[8,2048,512]{2,1,0:T(8,128)(2,1)}, bf16[8,512,512]{2,1,0:T(8,128)(2,1)}) custom-call(bf16[4,8,512,512]{3,2,1,0:T(8,128)(2,1)} %get-tuple-element.35.packed, bf16[2048,2048]{1,0:T(8,128)(2,1)} %get-tuple-element.36.mixed), custom_call_target="tpu_custom_call" | custom-call | tf_op jit(solution)/shard_map/cond/branch_3_fun/pallas_call | solution.py:328
  742.8 1.1 broadcast_in_dim.19.before
  743.9 19.5 %shard_map.79 = (bf16[8,512,512]{2,1,0:T(8,128)(2,1)}, f32[512,512]{1,0:T(8,128)}) custom-call(s32[8]{0:T(128)} %get-tuple-element.61.left_at, s32[8]{0:T(128)} %gather_fusion, s32[8]{0:T(128)} %get-tuple-element.73.kept.kept0, f32[8]{0:T(128)} %dynamic_slice.20.e_left, f32[8]{0:T(128)} %gather_fusion.2, bf16[8,2048,512]{2,1,0:T(8,128)(2,1)} %get-tuple-element.56.left, ...), custom_call_target="tpu_custom_call" | custom-call | flops 10737418240 | bytes 33554432 | tf_op jit(solution)/shard_map/pallas_call | solution.py:43
  763.4 17.5 %shard_map.80 = (bf16[8,512,512]{2,1,0:T(8,128)(2,1)}, f32[512,512]{1,0:T(8,128)}) custom-call(s32[8]{0:T(128)} %get-tuple-element.61.left_at, s32[8]{0:T(128)} %broadcast_minimum_fusion.right_at.at1, s32[8]{0:T(128)} %get-tuple-element.72.kept.kept1, f32[8]{0:T(128)} %dynamic_slice.20.e_left, f32[8]{0:T(128)} %gather_fusion.3, ...), custom_call_target="tpu_custom_call" | custom-call | flops 10737418240 | bytes 33554432 | tf_op jit(solution)/shard_map/pallas_call | solution.py:43
  780.9 2.3 copy.38
  783.3 30.0 %reduce-scatter.7.cloned.1.call-done = f32[8,1,16,512]{3,2,0,1:T(8,128)} async-done(((f32[8,4,16,512]{3,2,0,1:T(8,128)}), f32[8,1,16,512]{3,2,0,1:T(8,128)}) %reduce-scatter.7.cloned.1.call-update) | async-done | bytes 262160
  813.4 29.8 %shard_map.81 = bf16[2048,8,512]{2,1,0:T(8,128)(2,1)} custom-call(s32[8]{0:T(128)} %gather_fusion, s32[8]{0:T(128)} %broadcast_minimum_fusion.right_at.at1, s32[8]{0:T(128)} %get-tuple-element.73.kept.kept0, s32[8]{0:T(128)} %get-tuple-element.72.kept.kept1, bf16[8,2048,512]{2,1,0:T(8,128)(2,1)} %get-tuple-element.54.right.right0, ...), custom_call_target="tpu_custom_call" | custom-call | flops 17179869184 | bytes 50331648 | tf_op jit(solution)/shard_map/pallas_call | solution.py:106
  843.2 3.3 reduce-scatter.5.cloned.1.call-done
  846.5 17.2 %all-gather = f32[1,64,512]{2,1,0:T(8,128)S(1)} all-gather(f32[1,16,512]{2,1,0:T(8,128)} %reduce-scatter.5.cloned.1.call-done), channel_id=2, replica_groups=mesh['occ'=8,'aux'=4] {'aux'}, dimensions={1}, use_global_device_ids=true | all-gather | bytes 163840 | tf_op jit(solution)/shard_map/all_gather | solution.py:406
  863.7 0.7 multiply_bitcast_fusion
  (27 shorter events, 3.2 us)
Async XLA Ops:
  7.2 806.2 %reduce-scatter.7.cloned.1.call-start = ((), (), s32[]{:S(2)}) async-start(), calls=%async_computation.3 | async-start | bytes 1310720
  783.3 63.3 %reduce-scatter.5.cloned.1.call-start = ((), (), s32[]{:S(2)}) async-start(), calls=%async_computation.2 | async-start | bytes 294912 | tf_op jit(solution)/shard_map/reduce_scatter | solution.py:405
Sparse Core Ops, SparseCore 0:
  783.4 29.9 reduce-scatter.6
  815.6 30.8 reduce-scatter.4
